TPU v7x, 32 devices: a whole 2x2x4 slice. The times are simulated.
32 devices in a mesh: grp: 2 (over x), row: 16 (over z, y, core).
Axes of the slice: x: 2, y: 2, z: 4, core: 2. Of those that a mesh axis runs over, the one named last changes fastest.
Arguments:
- sequence_features: bfloat16 [256, 128, 64], P('grp', 'row'), parts along dimension 0, may hold values from -6 to 6
- edge_features: bfloat16 [256, 128, 128], P(('grp', 'row')), parts along dimension 0, may hold values from -6 to 6
- residue_features: bfloat16 [256, 384], P(('grp', 'row')), parts along dimension 0, may hold values from -6 to 6
- polymer_labels: int32 [256], P('grp'), parts along dimension 0, may hold values from 0 to 7, never falling along the last dimension, each value on 1 to 64 neighbouring positions
- polymer_membership: int32 [16, 128], P('grp'), parts along dimension 0, may hold values from 0 to 1, as said below
- present_residue_flags: int32 [256], P('grp'), parts along dimension 0, may hold values 0 or 1
- sequence_scaling_vector: float32 [64], replicated, may hold values from 0.1 to 1.9
- first_embedding_matrix: bfloat16 [64, 32], replicated, may hold values from -0.75 to 0.75
- second_embedding_matrix: bfloat16 [64, 32], replicated, may hold values from -0.75 to 0.75
- contraction_matrix: bfloat16 [1024, 128], replicated, may hold values from -0.375 to 0.375
- contraction_offset: float32 [128], replicated, may hold values from -3 to 3
- feedforward_scaling_vector: float32 [128], replicated, may hold values from 0.1 to 1.9
- feedforward_switch_matrix: bfloat16 [128, 512], replicated, may hold values from -0.5 to 0.5
- widening_matrix: bfloat16 [128, 512], replicated, may hold values from -0.5 to 0.5
- narrowing_matrix: bfloat16 [512, 128], replicated, may hold values from -0.25 to 0.25
- logit_scaling_vector: float32 [128], replicated, may hold values from 0.1 to 1.9
- edge_logit_matrix: bfloat16 [128, 16], replicated, may hold values from -2 to 2
- residue_scaling_vector: float32 [384], replicated, may hold values from 0.1 to 1.9
- asking_matrix: bfloat16 [384, 384], replicated, as said below
- lookup_matrix: bfloat16 [384, 384], replicated, as said below
- content_matrix: bfloat16 [384, 384], replicated, may hold values from -0.3125 to 0.3125
- heads_sigmoid_matrix: bfloat16 [384, 384], replicated, may hold values from -0.3125 to 0.3125
- heads_merge_matrix: bfloat16 [384, 384], replicated, may hold values from -0.3125 to 0.3125
Outputs:
- pair_out: bfloat16 [256, 128, 128], P(('grp', 'row')), parts along dimension 0
- single_out: bfloat16 [256, 384], P(('grp', 'row')), parts along dimension 0
There are 2 independent parts, one for each index of `grp`. A program takes and returns all parts, laid end to end along the dimension named above; an argument that names none is the same for every part. Nothing has to cross between parts.
Inputs may be any that keep to these rules, and one draw needn't show every extreme that they name: `polymer_labels`: never falling along the tokens. `polymer_membership`: entry [c, s] is 1 where chain c takes part in MSA row s; every chain takes part in exactly 64 rows. `present_residue_flags`: 1 marks a real token. `asking_matrix`: a real matrix. `lookup_matrix`: a real matrix.
All inputs are finite; a program needn't handle non-finite values.
Results may differ from a plain program's by a relative error of at most 0.012.
Values may be sent and summed in bfloat16 or wider, within the bound.
No kernel may reach another device: no remote copies, remote signals or barrier semaphores. Data moves between devices by JAX's collectives and lax.ppermute only.
A program may use at most 128 MiB of HBM per device.

v0:
```python
import math
import jax
import jax.numpy as jnp
from jax import lax
from jax.sharding import PartitionSpec as P

epsilon = 1e-05
highest = lax.Precision.HIGHEST


def standardize_features(values, scales):
    values = values.astype(jnp.float32)
    centred = values - jnp.mean(values, axis=-1, keepdims=True)
    spread = jnp.mean(centred * centred, axis=-1, keepdims=True)
    return centred * lax.rsqrt(spread + epsilon) * scales


def local(
    sequence_features,
    edge_features,
    residue_features,
    polymer_labels,
    polymer_membership,
    present_residue_flags,
    sequence_scaling_vector,
    first_embedding_matrix,
    second_embedding_matrix,
    contraction_matrix,
    contraction_offset,
    feedforward_scaling_vector,
    feedforward_switch_matrix,
    widening_matrix,
    narrowing_matrix,
    logit_scaling_vector,
    edge_logit_matrix,
    residue_scaling_vector,
    asking_matrix,
    lookup_matrix,
    content_matrix,
    heads_sigmoid_matrix,
    heads_merge_matrix,
):
    token_row_count = residue_features.shape[0]
    sequence_entries = sequence_features.shape[0]
    sequence_depth = sequence_features.shape[2]
    factor_channels_width = first_embedding_matrix.shape[1]
    pair_width = edge_features.shape[2]
    all_tokens = edge_features.shape[1]
    chains = polymer_membership.shape[0]
    heads = edge_logit_matrix.shape[1]
    single_width = residue_features.shape[1]
    head_size = single_width // heads
    first_token = lax.axis_index("row") * token_row_count
    onehot_all = (polymer_labels[:, None] == jnp.arange(chains, dtype=jnp.int32)[None, :]).astype(
        jnp.float32
    )
    onehot_mine = lax.dynamic_slice_in_dim(onehot_all, first_token, token_row_count, 0)
    pair_rows = polymer_membership.astype(jnp.float32)
    sequence_present_flags = jnp.dot(onehot_mine, pair_rows, precision=highest).T
    shared = jnp.dot(pair_rows, pair_rows.T, precision=highest)
    counts = jnp.dot(
        jnp.dot(onehot_mine, shared, precision=highest), onehot_all.T, precision=highest
    )
    standardized_sequences = standardize_features(
        sequence_features, sequence_scaling_vector
    ).astype(jnp.bfloat16)
    flattened_alignment = standardized_sequences.reshape(
        sequence_entries * token_row_count, sequence_depth
    )
    first_embedding_entries = (
        jnp.dot(
            flattened_alignment, first_embedding_matrix, preferred_element_type=jnp.float32
        ).reshape(sequence_entries, token_row_count, factor_channels_width)
        * sequence_present_flags[:, :, None]
    ).astype(jnp.bfloat16)
    left_flattened = first_embedding_entries.reshape(
        sequence_entries, token_row_count * factor_channels_width
    )
    second_embedding_entries = (
        jnp.dot(
            flattened_alignment, second_embedding_matrix, preferred_element_type=jnp.float32
        ).reshape(sequence_entries, token_row_count, factor_channels_width)
        * sequence_present_flags[:, :, None]
    ).astype(jnp.bfloat16)

    def finish_block(outer, column_start, stride_columns):
        shared_cols = lax.dynamic_slice_in_dim(counts, column_start, stride_columns, 1)
        outer = (outer / jnp.maximum(shared_cols, 1.0)[:, :, None]).astype(jnp.bfloat16)
        update = (
            jnp.dot(
                outer.reshape(
                    token_row_count * stride_columns, factor_channels_width * factor_channels_width
                ),
                contraction_matrix,
                preferred_element_type=jnp.float32,
            )
            + contraction_offset
        )
        old_cols = lax.dynamic_slice_in_dim(edge_features, column_start, stride_columns, 1).reshape(
            token_row_count * stride_columns, pair_width
        )
        return (
            (old_cols.astype(jnp.float32) + update)
            .astype(jnp.bfloat16)
            .reshape(token_row_count, stride_columns, pair_width)
        )

    factor_piece = lax.all_gather(second_embedding_entries, "row", axis=1, tiled=True)
    width = factor_piece.shape[1]
    stride_columns = math.gcd(width, 128)

    def one_block(offset):
        panel = lax.dynamic_slice_in_dim(factor_piece, offset, stride_columns, 1).reshape(
            sequence_entries, stride_columns * factor_channels_width
        )
        outer = lax.dot_general(
            left_flattened, panel, (((0,), (0,)), ((), ())), preferred_element_type=jnp.float32
        )
        outer = outer.reshape(
            token_row_count, factor_channels_width, stride_columns, factor_channels_width
        ).transpose(0, 2, 1, 3)
        outer = outer.reshape(
            token_row_count, stride_columns, factor_channels_width * factor_channels_width
        )
        return finish_block(outer, offset, stride_columns)

    blocks = lax.map(one_block, jnp.arange(0, width, stride_columns, dtype=jnp.int32))
    pair_one = blocks.transpose(1, 0, 2, 3).reshape(token_row_count, width, pair_width)
    flat_pair = pair_one.reshape(token_row_count * all_tokens, pair_width)
    normed_pair = standardize_features(flat_pair, feedforward_scaling_vector).astype(jnp.bfloat16)
    gated = jnp.dot(normed_pair, feedforward_switch_matrix, preferred_element_type=jnp.float32)
    lifted = jnp.dot(normed_pair, widening_matrix, preferred_element_type=jnp.float32)
    hidden = (jax.nn.silu(gated) * lifted).astype(jnp.bfloat16)
    pair_two = (
        flat_pair.astype(jnp.float32)
        + jnp.dot(hidden, narrowing_matrix, preferred_element_type=jnp.float32)
    ).astype(jnp.bfloat16)
    bias_normed = standardize_features(pair_two, logit_scaling_vector).astype(jnp.bfloat16)
    bias_rows = jnp.dot(bias_normed, edge_logit_matrix, preferred_element_type=jnp.float32)
    bias_heads = bias_rows.reshape(token_row_count, all_tokens, heads).transpose(2, 0, 1)
    pair_out = pair_two.reshape(token_row_count, all_tokens, pair_width)
    normed_single = standardize_features(residue_features, residue_scaling_vector).astype(
        jnp.bfloat16
    )
    query = jnp.dot(normed_single, asking_matrix, preferred_element_type=jnp.float32).astype(
        jnp.bfloat16
    )
    query_heads = query.reshape(token_row_count, heads, head_size)
    sigmoid_gate = jax.nn.sigmoid(
        jnp.dot(normed_single, heads_sigmoid_matrix, preferred_element_type=jnp.float32)
    )
    scale = 1.0 / math.sqrt(head_size)
    piece = lax.all_gather(normed_single, "row", axis=0, tiled=True)
    keys_piece = jnp.dot(piece, lookup_matrix, preferred_element_type=jnp.float32).astype(
        jnp.bfloat16
    )
    values_piece = jnp.dot(piece, content_matrix, preferred_element_type=jnp.float32).astype(
        jnp.bfloat16
    )
    width = keys_piece.shape[0]
    key_heads = keys_piece.reshape(width, heads, head_size)
    value_heads = values_piece.reshape(width, heads, head_size)
    scores = (
        jnp.einsum("ihd,jhd->hij", query_heads, key_heads, preferred_element_type=jnp.float32)
        * scale
    )
    scores = scores + bias_heads
    live = (present_residue_flags == 1)[None, None, :]
    scores = jnp.where(live, scores, -1e30)
    peak_old = jnp.full((heads, token_row_count), -1e30, jnp.float32)
    peak_new = jnp.maximum(peak_old, jnp.max(scores, axis=-1))
    expos = jnp.where(live, jnp.exp(scores - peak_new[:, :, None]), 0.0)
    total_new = jnp.sum(expos, axis=-1)
    accum_new = jnp.einsum(
        "hij,jhd->hid", expos.astype(jnp.bfloat16), value_heads, preferred_element_type=jnp.float32
    )
    mixed = accum_new / total_new[:, :, None]
    mixed = mixed.transpose(1, 0, 2).reshape(token_row_count, single_width)
    attended = (mixed * sigmoid_gate).astype(jnp.bfloat16)
    single_out = (
        residue_features.astype(jnp.float32)
        + jnp.dot(attended, heads_merge_matrix, preferred_element_type=jnp.float32)
    ).astype(jnp.bfloat16)
    return (pair_out, single_out)


def solution(mesh):
    placed = (
        P("grp", "row", None),
        P(("grp", "row"), None, None),
        P(("grp", "row"), None),
        P("grp"),
        P("grp", None),
        P("grp"),
        P(),
        P(),
        P(),
        P(),
        P(),
        P(),
        P(),
        P(),
        P(),
        P(),
        P(),
        P(),
        P(),
        P(),
        P(),
        P(),
        P(),
    )
    return jax.shard_map(
        local,
        mesh=mesh,
        in_specs=placed,
        out_specs=(P(("grp", "row"), None, None), P(("grp", "row"), None)),
        check_vma=False,
    )
```

profile of v0, /device:TPU:0, one launch (start us, length us, event | category | flops | bytes accessed | tf_op | source)
XLA Modules:
  0.0 77.5 jit_solution(2994039761496273403)
XLA Ops:
  7.3 0.8 %iota_compare_fusion = pred[128,8]{1,0:T(8,128)(4,1)S(1)} fusion(s32[128]{0:T(128)} %param.26), kind=kLoop, calls=%fused_computation.68 | loop fusion | flops 1024 | bytes 1536 | tf_op jit(solution)/shard_map/eq | solution.py:54
  8.1 0.9 %convert_reduce_fusion.1 = f32[128,8]{0,1:T(8,128)S(1)} fusion(bf16[128,8,64]{0,2,1:T(8,128)(2,1)} %param.23), kind=kLoop, calls=%fused_computation.50 | loop fusion | flops 130048 | bytes 135168 | tf_op jit(solution)/shard_map/reduce_sum | solution.py:13
  9.1 1.0 %fusion.42 = f32[128,8]{0,1:T(8,128)S(1)} fusion(bf16[128,8,64]{0,2,1:T(8,128)(2,1)} %param.23, f32[128,8]{0,1:T(8,128)S(1)} %broadcast_multiply_fusion.2), kind=kLoop, calls=%fused_computation.54 | loop fusion | flops 261120 | bytes 139264 | tf_op jit(solution)/shard_map/reduce_sum | solution.py:14
  10.1 0.8 %convolution_bitcast_fusion.3 = f32[128,8]{0,1:T(8,128)S(1)} fusion(s32[8,128]{1,0:T(8,128)} %param.27, pred[128,8]{1,0:T(8,128)(4,1)S(1)} %iota_compare_fusion, s32[]{:T(128)S(6)} %select_n.14), kind=kOutput, calls=%fused_computation.34 | convolution fusion | flops 99328 | bytes 9220 | tf_op jit(solution)/shard_map/dot_general | solution.py:59
  10.9 1.8 %fusion.19 = bf16[128,8,32]{0,2,1:T(8,128)(2,1)} fusion(f32[128,8]{0,1:T(8,128)S(1)} %convolution_bitcast_fusion.3, bf16[128,8,64]{0,2,1:T(8,128)(2,1)} %param.23, f32[64]{0:T(128)} %param.29, f32[128,8]{0,1:T(8,128)S(1)} %add_rsqrt_fusion.2, f32[128,8]{0,1:T(8,128)S(1)} %broadcast_multiply_fusion.2, bf16[64,32]{0,1:T(8,128)(2,1)} %param.31), kind=kOutput, calls=%fused_computation.17 | convolution fusion | flops 4587520 | bytes 213248 | tf_op jit(solution)/shard_map/dot_general | solution.py:80
  12.7 0.8 %convert_reduce_fusion.2 = f32[8]{0:T(128)S(1)} fusion(bf16[8,384]{1,0:T(8,128)(2,1)} %param.25), kind=kLoop, calls=%fused_computation.76 | loop fusion | flops 6136 | bytes 6176 | tf_op jit(solution)/shard_map/reduce_sum | solution.py:13
  13.5 0.9 %fusion.71 = f32[8]{0:T(128)S(1)} fusion(bf16[8,384]{1,0:T(8,128)(2,1)} %param.25, f32[8]{0:T(128)S(1)} %broadcast_multiply_fusion.3), kind=kLoop, calls=%fused_computation.79 | loop fusion | flops 12280 | bytes 6208 | tf_op jit(solution)/shard_map/reduce_sum | solution.py:14
  14.4 0.8 %fusion.73 = bf16[8,384]{1,0:T(8,128)(2,1)S(1)} fusion(bf16[8,384]{1,0:T(8,128)(2,1)} %param.25, f32[384]{0:T(512)} %param.40, f32[8]{0:T(128)S(1)} %add_rsqrt_fusion.3, f32[8]{0:T(128)S(1)} %broadcast_multiply_fusion.3), kind=kLoop, calls=%fused_computation.81 | loop fusion | flops 15360 | bytes 13888 | tf_op jit(solution)/shard_map/convert_element_type | solution.py:142
  15.1 23.4 %all_gather.7 = bf16[128,384]{1,0:T(8,128)(2,1)S(1)} all-gather(bf16[8,384]{1,0:T(8,128)(2,1)S(1)} %fusion.73), channel_id=1, replica_groups=mesh['grp'=2,'row'=16] {'row'}, dimensions={0}, use_global_device_ids=true | all-gather | bytes 104448 | tf_op jit(solution)/shard_map/all_gather | solution.py:153
  38.5 0.2 convolution_convert_fusion.1
  38.7 0.1 copy.36
  38.8 1.2 %convolution_convert_fusion.2 = bf16[8,384]{1,0:T(8,128)(2,1)S(1)} fusion(bf16[384,384]{1,0:T(8,128)(2,1)} %param.41, bf16[8,384]{1,0:T(8,128)(2,1)} %param.25, f32[384]{0:T(512)} %param.40, f32[8]{0:T(128)S(1)} %add_rsqrt_fusion.3, f32[8]{0:T(128)S(1)} %broadcast_multiply_fusion.3), kind=kOutput, calls=%fused_computation.33 | convolution fusion | flops 2377728 | bytes 308800 | tf_op jit(solution)/shard_map/dot_general | solution.py:145
  40.0 0.1 reshape.122
  40.2 1.2 %convolution_convert_fusion = bf16[128,384]{1,0:T(8,128)(2,1)S(1)} fusion(bf16[128,384]{1,0:T(8,128)(2,1)S(1)} %all_gather.7, bf16[384,384]{1,0:T(8,128)(2,1)} %param.43), kind=kOutput, calls=%fused_computation.12 | convolution fusion | flops 37797888 | bytes 491520 | tf_op jit(solution)/shard_map/dot_general | solution.py:157
  41.3 0.1 copy.38
  41.5 0.1 fusion.78
  41.6 0.1 fusion.81
  41.7 0.2 fusion.30
  42.0 11.4 %all-gather.2.cloned.1.call-done = bf16[128,128,32]{0,2,1:T(8,128)(2,1)} async-done(((bf16[128,8,32]{0,2,1:T(8,128)(2,1)}), bf16[128,128,32]{0,2,1:T(8,128)(2,1)}) %all-gather.2.cloned.1.call-update) | async-done | bytes 1048592 | tf_op jit(solution)/shard_map/all_gather | solution.py:108
  53.4 4.0 %convolution_bitcast_fusion = f32[8,128,32,32]{1,2,3,0:T(8,128)} fusion(bf16[128,32,128]{2,1,0:T(8,128)(2,1)} %bitcast.86, f32[128,8]{0,1:T(8,128)S(1)} %convolution_bitcast_fusion.3, bf16[128,8,64]{0,2,1:T(8,128)(2,1)S(1)} %copy-done.1, f32[64]{0:T(128)S(1)} %copy-done.8, f32[128,8]{0,1:T(8,128)S(1)} %add_rsqrt_fusion.2, ...), kind=kOutput, calls=%fused_computation.2 | convolution fusion | flops 273022976 | bytes 5390592 | tf_op jit(solution)/shard_map/while/body/eval_jaxpr/dot_general | solution.py:116
  57.5 4.7 %copy.35 = f32[8,128,32,32]{1,0,3,2:T(8,128)S(1)} copy(f32[8,128,32,32]{1,2,3,0:T(8,128)} %convolution_bitcast_fusion) | data formatting | bytes 8388608 | tf_op jit(solution)/shard_map/while/body/eval_jaxpr/transpose | solution.py:121
  62.2 1.3 %fusion.92 = (f32[1024]{0:T(1024)S(1)}, f32[1024,128]{1,0:T(8,128)S(1)}) fusion(f32[128]{0:T(128)S(1)} %copy-done.15, bf16[1024,128]{1,0:T(8,128)(2,1)S(1)} %copy-done.11, f32[128,8,8,128]{3,2,1,0:T(8,128)S(1)} %bitcast.85, f32[1024]{0:T(1024)S(1)} %fusion.30, bf16[1024,128]{1,0:T(8,128)(2,1)S(1)} %bitcast.92), kind=kOutput, calls=%fused_computation.106 | convolution fusion | flops 271318016 | bytes 5251584 | tf_op jit(solution)/shard_map/while/body/eval_jaxpr/dot_general | solution.py:90
  63.5 0.4 multiply_reduce_fusion
  63.9 0.5 fusion.41
  64.4 2.0 %convert_reduce_fusion = (f32[1024]{0:T(1024)S(1)}, bf16[1024,128]{1,0:T(8,128)(2,1)S(1)}) fusion(f32[1024,128]{1,0:T(8,128)S(1)} %get-tuple-element.19, bf16[512,128]{1,0:T(8,128)(2,1)} %param.37, f32[1024,512]{1,0:T(8,128)S(1)} %fusion.41, bf16[128,512]{1,0:T(8,128)(2,1)} %param.35, f32[128]{0:T(128)S(1)} %copy-done.9, f32[1024]{0:T(1024)S(1)} %add_rsqrt_fusion.1, ...), kind=kOutput, calls=%fused_computation.41 | convolution fusion | flops 272628736 | bytes 3158528 | tf_op jit(solution)/shard_map/dot_general | solution.py:136
  66.5 0.4 fusion.36
  66.9 0.9 %convolution_bitcast_fusion.2 = f32[2,8,8,128]{3,1,2,0:T(8,128)S(1)} fusion(bf16[128,16]{0,1:T(8,128)(2,1)S(1)} %copy-done.13, bf16[1024,128]{1,0:T(8,128)(2,1)S(1)} %get-tuple-element.21, f32[128]{0:T(128)S(1)} %copy-done.16, f32[1024]{0:T(1024)S(1)} %add_rsqrt_fusion, f32[1024]{0:T(1024)S(1)} %broadcast_multiply_fusion), kind=kOutput, calls=%fused_computation.21 | convolution fusion | flops 4849664 | bytes 340480 | tf_op jit(solution)/shard_map/dot_general | solution.py:139
  67.8 0.2 fusion.93
  68.1 0.2 fusion.59
  68.2 0.2 fusion.21
  68.5 0.1 reshape.126
  68.6 2.0 %fusion.29 = bf16[8,384]{1,0:T(8,128)(2,1)} fusion(bf16[384,384]{1,0:T(8,128)(2,1)} %param.45, f32[8,384]{1,0:T(8,128)S(1)} %reshape.126, bf16[384,384]{1,0:T(8,128)(2,1)} %param.44, bf16[8,384]{1,0:T(8,128)(2,1)S(1)} %copy-done.4, f32[384]{0:T(512)S(1)} %copy-done.7, f32[8]{0:T(128)S(1)} %add_rsqrt_fusion.3, f32[8]{0:T(128)S(1)} %broadcast_multiply_fusion.3), kind=kOutput, calls=%fused_computation.32 | convolution fusion | flops 4758528 | bytes 616000 | tf_op jit(solution)/shard_map/dot_general | solution.py:182
  (48 shorter events, 0.3 us)
Async XLA Ops:
  7.2 31.3 %copy-start = (bf16[384,384]{1,0:T(8,128)(2,1)S(1)}, bf16[384,384]{1,0:T(8,128)(2,1)}, u32[]{:S(2)}) copy-start(bf16[384,384]{1,0:T(8,128)(2,1)} %param.42) | copy-start | bytes 884740
  7.2 34.5 %copy-start.10 = (s32[128]{0:T(128)S(1)}, s32[128]{0:T(128)}, u32[]{:S(2)}) copy-start(s32[128]{0:T(128)} %param.26) | copy-start | bytes 1540
  7.2 46.2 %copy-start.1 = (bf16[128,8,64]{0,2,1:T(8,128)(2,1)S(1)}, bf16[128,8,64]{0,2,1:T(8,128)(2,1)}, u32[]{:S(2)}) copy-start(bf16[128,8,64]{0,2,1:T(8,128)(2,1)} %param.23) | copy-start | bytes 393220
  7.2 34.3 %copy-start.5 = (s32[8,128]{1,0:T(8,128)S(1)}, s32[8,128]{1,0:T(8,128)}, u32[]{:S(2)}) copy-start(s32[8,128]{1,0:T(8,128)} %param.27) | copy-start | bytes 12292
  7.2 46.2 %copy-start.8 = (f32[64]{0:T(128)S(1)}, f32[64]{0:T(128)}, u32[]{:S(2)}) copy-start(f32[64]{0:T(128)} %param.29) | copy-start | bytes 772
  7.2 34.7 %copy-start.14 = (s32[128]{0:T(128)S(1)}, s32[128]{0:T(128)}, u32[]{:S(2)}) copy-start(s32[128]{0:T(128)} %param.28) | copy-start | bytes 1540
  7.2 46.2 %copy-start.6 = (bf16[64,32]{0,1:T(8,128)(2,1)S(1)}, bf16[64,32]{0,1:T(8,128)(2,1)}, u32[]{:S(2)}) copy-start(bf16[64,32]{0,1:T(8,128)(2,1)} %param.30) | copy-start | bytes 12292
  7.2 46.2 %all-gather.2.cloned.1.call-start = ((), (), s32[]{:S(2)}) async-start(), calls=%async_computation | async-start | bytes 1114112 | tf_op jit(solution)/shard_map/all_gather | solution.py:108
  57.5 4.7 %copy-start.11 = (bf16[1024,128]{1,0:T(8,128)(2,1)S(1)}, bf16[1024,128]{1,0:T(8,128)(2,1)}, u32[]{:S(2)}) copy-start(bf16[1024,128]{1,0:T(8,128)(2,1)} %param.32) | copy-start | bytes 786436
  57.5 4.7 %copy-start.12 = (bf16[8,128,128]{2,1,0:T(8,128)(2,1)S(1)}, bf16[8,128,128]{2,1,0:T(8,128)(2,1)}, u32[]{:S(2)}) copy-start(bf16[8,128,128]{2,1,0:T(8,128)(2,1)} %param.24) | copy-start | bytes 786436
  57.5 4.7 %copy-start.15 = (f32[128]{0:T(128)S(1)}, f32[128]{0:T(128)}, u32[]{:S(2)}) copy-start(f32[128]{0:T(128)} %param.33) | copy-start | bytes 1540
  62.2 1.7 %copy-start.3 = (bf16[128,512]{1,0:T(8,128)(2,1)S(1)}, bf16[128,512]{1,0:T(8,128)(2,1)}, u32[]{:S(2)}) copy-start(bf16[128,512]{1,0:T(8,128)(2,1)} %param.36) | copy-start | bytes 393220
  62.2 1.7 %copy-start.9 = (f32[128]{0:T(128)S(1)}, f32[128]{0:T(128)}, u32[]{:S(2)}) copy-start(f32[128]{0:T(128)} %param.34) | copy-start | bytes 1540
  64.4 2.5 %copy-start.13 = (bf16[128,16]{0,1:T(8,128)(2,1)S(1)}, bf16[128,16]{0,1:T(8,128)(2,1)}, u32[]{:S(2)}) copy-start(bf16[128,16]{0,1:T(8,128)(2,1)} %param.39) | copy-start | bytes 12292
  64.4 2.5 %copy-start.16 = (f32[128]{0:T(128)S(1)}, f32[128]{0:T(128)}, u32[]{:S(2)}) copy-start(f32[128]{0:T(128)} %param.38) | copy-start | bytes 1540
  64.4 4.2 %copy-start.4 = (bf16[8,384]{1,0:T(8,128)(2,1)S(1)}, bf16[8,384]{1,0:T(8,128)(2,1)}, u32[]{:S(2)}) copy-start(bf16[8,384]{1,0:T(8,128)(2,1)} %param.25) | copy-start | bytes 18436
  64.4 4.2 %copy-start.7 = (f32[384]{0:T(512)S(1)}, f32[384]{0:T(512)}, u32[]{:S(2)}) copy-start(f32[384]{0:T(512)} %param.40) | copy-start | bytes 4612
  66.5 4.1 %copy-start.2 = (bf16[1024,128]{1,0:T(8,128)(2,1)}, bf16[1024,128]{1,0:T(8,128)(2,1)S(1)}, u32[]{:S(2)}) copy-start(bf16[1024,128]{1,0:T(8,128)(2,1)S(1)} %get-tuple-element.21) | copy-start | bytes 786436
Sparse Core Ops, SparseCore 0:
  12.8 40.5 all-gather.1
where the time goes:
time: 77.9 us; the launch traced here: 77.5 us
  blocking collectives  23.4 us (30%)
  matrix products  16.8 us (22%)
  between operations  14.4 us (18%)
  waiting for transfers between devices  11.4 us (15%)
  other arithmetic  6.2 us (8%)
  local copies, waits for them, and re-layouts  5.24 us (7%)
    all_gather x1, blocking collectives, local(): piece = lax.all_gather(normed_single, 'row', axis=0, tiled=True)  23.4 us
    all_gather x1, waiting for transfers between devices, local(): lax.all_gather(second_embedding_entries, 'row', axis=1, tiled=True)  11.4 us
    transpose x1, local copies, waits for them, and re-layouts, one_block(): outer = outer.reshape(token_row_count, factor_channels_width, stride_colu...  4.68 us
    dot_general x1, matrix products, one_block(): lax.dot_general(left_flattened, panel, (((0,), (0,)), ((), ())), preferre...  4.04 us
    reduce_sum x4, other arithmetic, standardize_features(): spread = jnp.mean(centred * centred, axis=-1, keepdims=True)  2.55 us
    dot_general x1, matrix products, local(): jnp.dot(hidden, narrowing_matrix, preferred_element_type=jnp.float32)  2.04 us
    dot_general x1, matrix products, local(): jnp.dot(attended, heads_merge_matrix, preferred_element_type=jnp.float32)  2 us
    dot_general x1, matrix products, local(): jnp.dot(flattened_alignment, second_embedding_matrix, preferred_element_t...  1.76 us
  transfers between devices with their start and end apart: 1, of which 1 were waited for; matrix products, arithmetic and copies ran while one was open for 8% of the time, Pallas kernels for 0%

commit v1 on v0

--- a/solution.py
+++ b/solution.py
@@ -6,6 +6,16 @@
 
 epsilon = 1e-05
 highest = lax.Precision.HIGHEST
+
+
+def gather_by_hops(x, axis, dim):
+    size = lax.axis_size(axis)
+    moving, blocks = (x, [x])
+    for _ in range(size - 1):
+        moving = lax.ppermute(moving, axis, [(i, (i + 1) % size) for i in range(size)])
+        blocks.insert(0, moving)
+    line = jnp.concatenate(blocks, axis=dim)
+    return jnp.roll(line, (lax.axis_index(axis) + 1) * x.shape[dim], axis=dim)
 
 
 def standardize_features(values, scales):
@@ -105,7 +115,7 @@
             .reshape(token_row_count, stride_columns, pair_width)
         )
 
-    factor_piece = lax.all_gather(second_embedding_entries, "row", axis=1, tiled=True)
+    factor_piece = gather_by_hops(second_embedding_entries, "row", 1)
     width = factor_piece.shape[1]
     stride_columns = math.gcd(width, 128)
 

time: 77.9 us -> 132 us (1.69)
  waiting for transfers between devices: 11.4 us -> 84.7 us
  between operations: 14.4 us -> 1.16 us
  blocking collectives: 23.4 us -> 18.2 us
  matrix products: 16.8 us -> 14.9 us
    ppermute x0 -> x15, waiting for transfers between devices: none -> 84.7 us  [gather_by_hops(): lax.ppermute(moving, axis, [(i, (i + 1) % size) for i in range(size)])]
    all_gather x1 -> x0, waiting for transfers between devices: 11.4 us -> none  [local(): lax.all_gather(second_embedding_entries, 'row', axis=1, tiled=True)]
    all_gather x1, blocking collectives: 23.4 us -> 18.2 us  [local(): piece = lax.all_gather(normed_single, 'row', axis=0, tiled=True)]
  transfers between devices with their start and end apart: 1 -> 15, of which waited for: 1 -> 14; matrix products, arithmetic and copies ran while one was open for 8% -> 4% of each run, Pallas kernels for 0% -> 0%
where the time goes in v1:
time: 132 us
  waiting for transfers between devices  84.7 us (64%)
  blocking collectives  18.2 us (14%)
  matrix products  14.9 us (11%)
  local copies, waits for them, and re-layouts  6.24 us (5%)
  other arithmetic  6.07 us (5%)
    ppermute x15, waiting for transfers between devices, gather_by_hops(): lax.ppermute(moving, axis, [(i, (i + 1) % size) for i in range(size)])  84.7 us
    all_gather x1, blocking collectives, local(): piece = lax.all_gather(normed_single, 'row', axis=0, tiled=True)  18.2 us
    transpose x1, local copies, waits for them, and re-layouts, one_block(): outer = outer.reshape(token_row_count, factor_channels_width, stride_colu...  4.68 us
    dot_general x1, matrix products, one_block(): lax.dot_general(left_flattened, panel, (((0,), (0,)), ((), ())), preferre...  2.82 us
  transfers between devices with their start and end apart: 15, of which 14 were waited for; matrix products, arithmetic and copies ran while one was open for 4% of the time, Pallas kernels for 0%

profile of v1, /device:TPU:0, one launch (start us, length us, event | category | flops | bytes accessed | tf_op | source)
XLA Modules:
  0.0 132.1 jit_solution(6625230283193086518)
XLA Ops:
  0.7 0.8 iota_compare_fusion
  1.5 0.9 convert_reduce_fusion.1
  2.4 1.0 fusion.42
  3.4 0.8 convolution_bitcast_fusion.3
  4.2 1.1 fusion.19
  5.3 0.5 collective-permute-start
  5.9 6.9 %collective-permute-done = bf16[128,8,32]{0,2,1:T(8,128)(2,1)S(1)} collective-permute-done((bf16[128,8,32]{0,2,1:T(8,128)(2,1)S(1)}, bf16[128,8,32]{0,2,1:T(8,128)(2,1)S(1)}, u32[]{:S(2)}, u32[]{:S(2)}) %collective-permute-start) | collective-permute-done | bytes 65568 | tf_op jit(solution)/shard_map/ppermute | solution.py:15
  12.8 6.4 %collective-permute-done.1 = bf16[128,8,32]{0,2,1:T(8,128)(2,1)S(1)} collective-permute-done((bf16[128,8,32]{0,2,1:T(8,128)(2,1)S(1)}, bf16[128,8,32]{0,2,1:T(8,128)(2,1)S(1)}, u32[]{:S(2)}, u32[]{:S(2)}) %collective-permute-start.1) | collective-permute-done | bytes 65568 | tf_op jit(solution)/shard_map/ppermute | solution.py:15
  19.2 6.4 %collective-permute-done.2 = bf16[128,8,32]{0,2,1:T(8,128)(2,1)S(1)} collective-permute-done((bf16[128,8,32]{0,2,1:T(8,128)(2,1)S(1)}, bf16[128,8,32]{0,2,1:T(8,128)(2,1)S(1)}, u32[]{:S(2)}, u32[]{:S(2)}) %collective-permute-start.2) | collective-permute-done | bytes 65568 | tf_op jit(solution)/shard_map/ppermute | solution.py:15
  25.6 0.8 convert_reduce_fusion.2
  26.4 5.6 %collective-permute-done.3 = bf16[128,8,32]{0,2,1:T(8,128)(2,1)S(1)} collective-permute-done((bf16[128,8,32]{0,2,1:T(8,128)(2,1)S(1)}, bf16[128,8,32]{0,2,1:T(8,128)(2,1)S(1)}, u32[]{:S(2)}, u32[]{:S(2)}) %collective-permute-start.3) | collective-permute-done | bytes 65568 | tf_op jit(solution)/shard_map/ppermute | solution.py:15
  32.0 6.4 %collective-permute-done.4 = bf16[128,8,32]{0,2,1:T(8,128)(2,1)S(1)} collective-permute-done((bf16[128,8,32]{0,2,1:T(8,128)(2,1)S(1)}, bf16[128,8,32]{0,2,1:T(8,128)(2,1)S(1)}, u32[]{:S(2)}, u32[]{:S(2)}) %collective-permute-start.4) | collective-permute-done | bytes 65568 | tf_op jit(solution)/shard_map/ppermute | solution.py:15
  38.4 0.9 fusion.71
  39.2 5.5 %collective-permute-done.5 = bf16[128,8,32]{0,2,1:T(8,128)(2,1)S(1)} collective-permute-done((bf16[128,8,32]{0,2,1:T(8,128)(2,1)S(1)}, bf16[128,8,32]{0,2,1:T(8,128)(2,1)S(1)}, u32[]{:S(2)}, u32[]{:S(2)}) %collective-permute-start.5) | collective-permute-done | bytes 65568 | tf_op jit(solution)/shard_map/ppermute | solution.py:15
  44.8 6.4 %collective-permute-done.6 = bf16[128,8,32]{0,2,1:T(8,128)(2,1)S(1)} collective-permute-done((bf16[128,8,32]{0,2,1:T(8,128)(2,1)S(1)}, bf16[128,8,32]{0,2,1:T(8,128)(2,1)S(1)}, u32[]{:S(2)}, u32[]{:S(2)}) %collective-permute-start.6) | collective-permute-done | bytes 65568 | tf_op jit(solution)/shard_map/ppermute | solution.py:15
  51.1 0.8 fusion.73
  51.9 18.2 %all_gather.3 = bf16[128,384]{1,0:T(8,128)(2,1)S(1)} all-gather(bf16[8,384]{1,0:T(8,128)(2,1)S(1)} %fusion.73), channel_id=1, replica_groups=mesh['grp'=2,'row'=16] {'row'}, dimensions={0}, use_global_device_ids=true | all-gather | bytes 104448 | tf_op jit(solution)/shard_map/all_gather | solution.py:163
  70.5 6.0 %collective-permute-done.8 = bf16[128,8,32]{0,2,1:T(8,128)(2,1)S(1)} collective-permute-done((bf16[128,8,32]{0,2,1:T(8,128)(2,1)S(1)}, bf16[128,8,32]{0,2,1:T(8,128)(2,1)S(1)}, u32[]{:S(2)}, u32[]{:S(2)}) %collective-permute-start.8) | collective-permute-done | bytes 65568 | tf_op jit(solution)/shard_map/ppermute | solution.py:15
  76.6 1.2 convolution_convert_fusion
  77.7 5.2 %collective-permute-done.9 = bf16[128,8,32]{0,2,1:T(8,128)(2,1)S(1)} collective-permute-done((bf16[128,8,32]{0,2,1:T(8,128)(2,1)S(1)}, bf16[128,8,32]{0,2,1:T(8,128)(2,1)S(1)}, u32[]{:S(2)}, u32[]{:S(2)}) %collective-permute-start.9) | collective-permute-done | bytes 65568 | tf_op jit(solution)/shard_map/ppermute | solution.py:15
  82.9 1.2 convolution_convert_fusion.2
  84.1 5.2 %collective-permute-done.10 = bf16[128,8,32]{0,2,1:T(8,128)(2,1)S(1)} collective-permute-done((bf16[128,8,32]{0,2,1:T(8,128)(2,1)S(1)}, bf16[128,8,32]{0,2,1:T(8,128)(2,1)S(1)}, u32[]{:S(2)}, u32[]{:S(2)}) %collective-permute-start.10) | collective-permute-done | bytes 65568 | tf_op jit(solution)/shard_map/ppermute | solution.py:15
  89.5 6.3 %collective-permute-done.11 = bf16[128,8,32]{0,2,1:T(8,128)(2,1)S(1)} collective-permute-done((bf16[128,8,32]{0,2,1:T(8,128)(2,1)S(1)}, bf16[128,8,32]{0,2,1:T(8,128)(2,1)S(1)}, u32[]{:S(2)}, u32[]{:S(2)}) %collective-permute-start.11) | collective-permute-done | bytes 65568 | tf_op jit(solution)/shard_map/ppermute | solution.py:15
  95.8 6.3 %collective-permute-done.12 = bf16[128,8,32]{0,2,1:T(8,128)(2,1)S(1)} collective-permute-done((bf16[128,8,32]{0,2,1:T(8,128)(2,1)S(1)}, bf16[128,8,32]{0,2,1:T(8,128)(2,1)S(1)}, u32[]{:S(2)}, u32[]{:S(2)}) %collective-permute-start.12) | collective-permute-done | bytes 65568 | tf_op jit(solution)/shard_map/ppermute | solution.py:15
  102.5 6.0 %collective-permute-done.13 = bf16[128,8,32]{0,2,1:T(8,128)(2,1)S(1)} collective-permute-done((bf16[128,8,32]{0,2,1:T(8,128)(2,1)S(1)}, bf16[128,8,32]{0,2,1:T(8,128)(2,1)S(1)}, u32[]{:S(2)}, u32[]{:S(2)}) %collective-permute-start.13) | collective-permute-done | bytes 65568 | tf_op jit(solution)/shard_map/ppermute | solution.py:15
  108.7 6.2 %collective-permute-done.14 = bf16[128,8,32]{0,2,1:T(8,128)(2,1)S(1)} collective-permute-done((bf16[128,8,32]{0,2,1:T(8,128)(2,1)S(1)}, bf16[128,8,32]{0,2,1:T(8,128)(2,1)S(1)}, u32[]{:S(2)}, u32[]{:S(2)}) %collective-permute-start.14) | collective-permute-done | bytes 65568 | tf_op jit(solution)/shard_map/ppermute | solution.py:15
  116.1 2.8 %convolution_bitcast_fusion = f32[8,128,32,32]{1,2,3,0:T(8,128)} fusion(bf16[128,32,128]{2,1,0:T(8,128)(2,1)S(1)} %dynamic-slice_bitcast_fusion, f32[128,8]{0,1:T(8,128)S(1)} %convolution_bitcast_fusion.3, bf16[128,8,64]{0,2,1:T(8,128)(2,1)S(1)} %copy-done.1, f32[64]{0:T(128)S(1)} %copy-done.8, f32[128,8]{0,1:T(8,128)S(1)} %add_rsqrt_fusion.2, ...), kind=kOutput, calls=%fused_computation.2 | convolution fusion | flops 273022976 | bytes 5390592 | tf_op jit(solution)/shard_map/while/body/eval_jaxpr/dot_general | solution.py:126
  118.9 4.7 %copy.29 = f32[8,128,32,32]{1,0,3,2:T(8,128)S(1)} copy(f32[8,128,32,32]{1,2,3,0:T(8,128)} %convolution_bitcast_fusion) | data formatting | bytes 8388608 | tf_op jit(solution)/shard_map/while/body/eval_jaxpr/transpose | solution.py:131
  123.6 1.3 fusion.92
  125.9 2.0 %convert_reduce_fusion = (f32[1024]{0:T(1024)S(1)}, bf16[1024,128]{1,0:T(8,128)(2,1)S(1)}) fusion(f32[1024,128]{1,0:T(8,128)S(1)} %get-tuple-element.19, bf16[512,128]{1,0:T(8,128)(2,1)} %param.37, f32[1024,512]{1,0:T(8,128)S(1)} %fusion.41, bf16[128,512]{1,0:T(8,128)(2,1)} %param.35, f32[128]{0:T(128)S(1)} %copy-done.9, f32[1024]{0:T(1024)S(1)} %add_rsqrt_fusion.1, ...), kind=kOutput, calls=%fused_computation.42 | convolution fusion | flops 272628736 | bytes 3158528 | tf_op jit(solution)/shard_map/dot_general | solution.py:146
  128.3 0.9 convolution_bitcast_fusion.2
  130.0 2.0 %fusion.29 = bf16[8,384]{1,0:T(8,128)(2,1)} fusion(bf16[384,384]{1,0:T(8,128)(2,1)} %param.45, f32[8,384]{1,0:T(8,128)S(1)} %reshape.126, bf16[384,384]{1,0:T(8,128)(2,1)} %param.44, bf16[8,384]{1,0:T(8,128)(2,1)S(1)} %copy-done.4, f32[384]{0:T(512)S(1)} %copy-done.7, f32[8]{0:T(128)S(1)} %add_rsqrt_fusion.3, f32[8]{0:T(128)S(1)} %broadcast_multiply_fusion.3), kind=kOutput, calls=%fused_computation.32 | convolution fusion | flops 4758528 | bytes 616000 | tf_op jit(solution)/shard_map/dot_general | solution.py:192
  (108 shorter events, 4.3 us)
Async XLA Ops:
  0.6 69.7 %copy-start = (bf16[384,384]{1,0:T(8,128)(2,1)S(1)}, bf16[384,384]{1,0:T(8,128)(2,1)}, u32[]{:S(2)}) copy-start(bf16[384,384]{1,0:T(8,128)(2,1)} %param.42) | copy-start | bytes 884740
  0.6 107.9 %copy-start.10 = (s32[128]{0:T(128)S(1)}, s32[128]{0:T(128)}, u32[]{:S(2)}) copy-start(s32[128]{0:T(128)} %param.26) | copy-start | bytes 1540
  0.7 88.7 %copy-start.5 = (s32[8,128]{1,0:T(8,128)S(1)}, s32[8,128]{1,0:T(8,128)}, u32[]{:S(2)}) copy-start(s32[8,128]{1,0:T(8,128)} %param.27) | copy-start | bytes 12292
  0.7 101.4 %copy-start.14 = (s32[128]{0:T(128)S(1)}, s32[128]{0:T(128)}, u32[]{:S(2)}) copy-start(s32[128]{0:T(128)} %param.28) | copy-start | bytes 1540
  5.3 7.5 %collective-permute-start = (bf16[128,8,32]{0,2,1:T(8,128)(2,1)S(1)}, bf16[128,8,32]{0,2,1:T(8,128)(2,1)S(1)}, u32[]{:S(2)}, u32[]{:S(2)}) collective-permute-start(bf16[128,8,32]{0,2,1:T(8,128)(2,1)S(1)} %fusion.19), channel_id=1, source_target_pairs={{0,1},{1,2},{2,3},{3,4},{4,5},{5,6},{6,7},{7,8},{8,9},{9,10},{10,1... | collective-permute-start | bytes 196616 | tf_op jit(solution)/shard_map/ppermute | solution.py:15
  12.8 6.4 %collective-permute-start.1 = (bf16[128,8,32]{0,2,1:T(8,128)(2,1)S(1)}, bf16[128,8,32]{0,2,1:T(8,128)(2,1)S(1)}, u32[]{:S(2)}, u32[]{:S(2)}) collective-permute-start(bf16[128,8,32]{0,2,1:T(8,128)(2,1)S(1)} %collective-permute-done), channel_id=1, source_target_pairs={{0,1},{1,2},{2,3},{3,4},{4,5},{5,6},{6,7},{7,8},{8,9},{9,10},{10,1... | collective-permute-start | bytes 196616 | tf_op jit(solution)/shard_map/ppermute | solution.py:15
  19.2 6.4 %collective-permute-start.2 = (bf16[128,8,32]{0,2,1:T(8,128)(2,1)S(1)}, bf16[128,8,32]{0,2,1:T(8,128)(2,1)S(1)}, u32[]{:S(2)}, u32[]{:S(2)}) collective-permute-start(bf16[128,8,32]{0,2,1:T(8,128)(2,1)S(1)} %collective-permute-done.1), channel_id=1, source_target_pairs={{0,1},{1,2},{2,3},{3,4},{4,5},{5,6},{6,7},{7,8},{8,9},{9,10},{10,1... | collective-permute-start | bytes 196616 | tf_op jit(solution)/shard_map/ppermute | solution.py:15
  25.6 6.4 %collective-permute-start.3 = (bf16[128,8,32]{0,2,1:T(8,128)(2,1)S(1)}, bf16[128,8,32]{0,2,1:T(8,128)(2,1)S(1)}, u32[]{:S(2)}, u32[]{:S(2)}) collective-permute-start(bf16[128,8,32]{0,2,1:T(8,128)(2,1)S(1)} %collective-permute-done.2), channel_id=1, source_target_pairs={{0,1},{1,2},{2,3},{3,4},{4,5},{5,6},{6,7},{7,8},{8,9},{9,10},{10,1... | collective-permute-start | bytes 196616 | tf_op jit(solution)/shard_map/ppermute | solution.py:15
  32.0 6.4 %collective-permute-start.4 = (bf16[128,8,32]{0,2,1:T(8,128)(2,1)S(1)}, bf16[128,8,32]{0,2,1:T(8,128)(2,1)S(1)}, u32[]{:S(2)}, u32[]{:S(2)}) collective-permute-start(bf16[128,8,32]{0,2,1:T(8,128)(2,1)S(1)} %collective-permute-done.3), channel_id=1, source_target_pairs={{0,1},{1,2},{2,3},{3,4},{4,5},{5,6},{6,7},{7,8},{8,9},{9,10},{10,1... | collective-permute-start | bytes 196616 | tf_op jit(solution)/shard_map/ppermute | solution.py:15
  38.4 6.4 %collective-permute-start.5 = (bf16[128,8,32]{0,2,1:T(8,128)(2,1)S(1)}, bf16[128,8,32]{0,2,1:T(8,128)(2,1)S(1)}, u32[]{:S(2)}, u32[]{:S(2)}) collective-permute-start(bf16[128,8,32]{0,2,1:T(8,128)(2,1)S(1)} %collective-permute-done.4), channel_id=1, source_target_pairs={{0,1},{1,2},{2,3},{3,4},{4,5},{5,6},{6,7},{7,8},{8,9},{9,10},{10,1... | collective-permute-start | bytes 196616 | tf_op jit(solution)/shard_map/ppermute | solution.py:15
  44.8 6.4 %collective-permute-start.6 = (bf16[128,8,32]{0,2,1:T(8,128)(2,1)S(1)}, bf16[128,8,32]{0,2,1:T(8,128)(2,1)S(1)}, u32[]{:S(2)}, u32[]{:S(2)}) collective-permute-start(bf16[128,8,32]{0,2,1:T(8,128)(2,1)S(1)} %collective-permute-done.5), channel_id=1, source_target_pairs={{0,1},{1,2},{2,3},{3,4},{4,5},{5,6},{6,7},{7,8},{8,9},{9,10},{10,1... | collective-permute-start | bytes 196616 | tf_op jit(solution)/shard_map/ppermute | solution.py:15
  51.1 19.0 %collective-permute-start.7 = (bf16[128,8,32]{0,2,1:T(8,128)(2,1)S(1)}, bf16[128,8,32]{0,2,1:T(8,128)(2,1)S(1)}, u32[]{:S(2)}, u32[]{:S(2)}) collective-permute-start(bf16[128,8,32]{0,2,1:T(8,128)(2,1)S(1)} %collective-permute-done.6), channel_id=1, source_target_pairs={{0,1},{1,2},{2,3},{3,4},{4,5},{5,6},{6,7},{7,8},{8,9},{9,10},{10,1... | collective-permute-start | bytes 196616 | tf_op jit(solution)/shard_map/ppermute | solution.py:15
  70.2 6.4 %collective-permute-start.8 = (bf16[128,8,32]{0,2,1:T(8,128)(2,1)S(1)}, bf16[128,8,32]{0,2,1:T(8,128)(2,1)S(1)}, u32[]{:S(2)}, u32[]{:S(2)}) collective-permute-start(bf16[128,8,32]{0,2,1:T(8,128)(2,1)S(1)} %collective-permute-done.7), channel_id=1, source_target_pairs={{0,1},{1,2},{2,3},{3,4},{4,5},{5,6},{6,7},{7,8},{8,9},{9,10},{10,1... | collective-permute-start | bytes 196616 | tf_op jit(solution)/shard_map/ppermute | solution.py:15
  76.5 6.4 %collective-permute-start.9 = (bf16[128,8,32]{0,2,1:T(8,128)(2,1)S(1)}, bf16[128,8,32]{0,2,1:T(8,128)(2,1)S(1)}, u32[]{:S(2)}, u32[]{:S(2)}) collective-permute-start(bf16[128,8,32]{0,2,1:T(8,128)(2,1)S(1)} %collective-permute-done.8), channel_id=1, source_target_pairs={{0,1},{1,2},{2,3},{3,4},{4,5},{5,6},{6,7},{7,8},{8,9},{9,10},{10,1... | collective-permute-start | bytes 196616 | tf_op jit(solution)/shard_map/ppermute | solution.py:15
  82.9 6.4 %collective-permute-start.10 = (bf16[128,8,32]{0,2,1:T(8,128)(2,1)S(1)}, bf16[128,8,32]{0,2,1:T(8,128)(2,1)S(1)}, u32[]{:S(2)}, u32[]{:S(2)}) collective-permute-start(bf16[128,8,32]{0,2,1:T(8,128)(2,1)S(1)} %collective-permute-done.9), channel_id=1, source_target_pairs={{0,1},{1,2},{2,3},{3,4},{4,5},{5,6},{6,7},{7,8},{8,9},{9,10},{10,1... | collective-permute-start | bytes 196616 | tf_op jit(solution)/shard_map/ppermute | solution.py:15
  89.3 6.4 %collective-permute-start.11 = (bf16[128,8,32]{0,2,1:T(8,128)(2,1)S(1)}, bf16[128,8,32]{0,2,1:T(8,128)(2,1)S(1)}, u32[]{:S(2)}, u32[]{:S(2)}) collective-permute-start(bf16[128,8,32]{0,2,1:T(8,128)(2,1)S(1)} %collective-permute-done.10), channel_id=1, source_target_pairs={{0,1},{1,2},{2,3},{3,4},{4,5},{5,6},{6,7},{7,8},{8,9},{9,10},{10,1... | collective-permute-start | bytes 196616 | tf_op jit(solution)/shard_map/ppermute | solution.py:15
  95.7 6.4 %collective-permute-start.12 = (bf16[128,8,32]{0,2,1:T(8,128)(2,1)S(1)}, bf16[128,8,32]{0,2,1:T(8,128)(2,1)S(1)}, u32[]{:S(2)}, u32[]{:S(2)}) collective-permute-start(bf16[128,8,32]{0,2,1:T(8,128)(2,1)S(1)} %collective-permute-done.11), channel_id=1, source_target_pairs={{0,1},{1,2},{2,3},{3,4},{4,5},{5,6},{6,7},{7,8},{8,9},{9,10},{10,1... | collective-permute-start | bytes 196616 | tf_op jit(solution)/shard_map/ppermute | solution.py:15
  102.1 6.4 %collective-permute-start.13 = (bf16[128,8,32]{0,2,1:T(8,128)(2,1)S(1)}, bf16[128,8,32]{0,2,1:T(8,128)(2,1)S(1)}, u32[]{:S(2)}, u32[]{:S(2)}) collective-permute-start(bf16[128,8,32]{0,2,1:T(8,128)(2,1)S(1)} %collective-permute-done.12), channel_id=1, source_target_pairs={{0,1},{1,2},{2,3},{3,4},{4,5},{5,6},{6,7},{7,8},{8,9},{9,10},{10,1... | collective-permute-start | bytes 196616 | tf_op jit(solution)/shard_map/ppermute | solution.py:15
  108.5 6.4 %collective-permute-start.14 = (bf16[128,8,32]{0,2,1:T(8,128)(2,1)S(1)}, bf16[128,8,32]{0,2,1:T(8,128)(2,1)S(1)}, u32[]{:S(2)}, u32[]{:S(2)}) collective-permute-start(bf16[128,8,32]{0,2,1:T(8,128)(2,1)S(1)} %collective-permute-done.13), channel_id=1, source_target_pairs={{0,1},{1,2},{2,3},{3,4},{4,5},{5,6},{6,7},{7,8},{8,9},{9,10},{10,1... | collective-permute-start | bytes 196616 | tf_op jit(solution)/shard_map/ppermute | solution.py:15
  115.2 0.9 copy-start.1
  115.2 0.9 copy-start.6
  115.2 0.9 copy-start.8
  118.9 4.7 %copy-start.11 = (bf16[1024,128]{1,0:T(8,128)(2,1)S(1)}, bf16[1024,128]{1,0:T(8,128)(2,1)}, u32[]{:S(2)}) copy-start(bf16[1024,128]{1,0:T(8,128)(2,1)} %param.32) | copy-start | bytes 786436
  118.9 4.7 %copy-start.12 = (bf16[8,128,128]{2,1,0:T(8,128)(2,1)S(1)}, bf16[8,128,128]{2,1,0:T(8,128)(2,1)}, u32[]{:S(2)}) copy-start(bf16[8,128,128]{2,1,0:T(8,128)(2,1)} %param.24) | copy-start | bytes 786436
  118.9 4.7 %copy-start.15 = (f32[128]{0:T(128)S(1)}, f32[128]{0:T(128)}, u32[]{:S(2)}) copy-start(f32[128]{0:T(128)} %param.33) | copy-start | bytes 1540
  123.6 1.7 %copy-start.3 = (bf16[128,512]{1,0:T(8,128)(2,1)S(1)}, bf16[128,512]{1,0:T(8,128)(2,1)}, u32[]{:S(2)}) copy-start(bf16[128,512]{1,0:T(8,128)(2,1)} %param.36) | copy-start | bytes 393220
  123.6 1.7 %copy-start.9 = (f32[128]{0:T(128)S(1)}, f32[128]{0:T(128)}, u32[]{:S(2)}) copy-start(f32[128]{0:T(128)} %param.34) | copy-start | bytes 1540
  125.8 2.5 %copy-start.13 = (bf16[128,16]{0,1:T(8,128)(2,1)S(1)}, bf16[128,16]{0,1:T(8,128)(2,1)}, u32[]{:S(2)}) copy-start(bf16[128,16]{0,1:T(8,128)(2,1)} %param.39) | copy-start | bytes 12292
  125.8 2.5 %copy-start.16 = (f32[128]{0:T(128)S(1)}, f32[128]{0:T(128)}, u32[]{:S(2)}) copy-start(f32[128]{0:T(128)} %param.38) | copy-start | bytes 1540
  125.8 4.2 %copy-start.4 = (bf16[8,384]{1,0:T(8,128)(2,1)S(1)}, bf16[8,384]{1,0:T(8,128)(2,1)}, u32[]{:S(2)}) copy-start(bf16[8,384]{1,0:T(8,128)(2,1)} %param.25) | copy-start | bytes 18436
  125.8 4.2 %copy-start.7 = (f32[384]{0:T(512)S(1)}, f32[384]{0:T(512)}, u32[]{:S(2)}) copy-start(f32[384]{0:T(512)} %param.40) | copy-start | bytes 4612
  127.9 4.1 %copy-start.2 = (bf16[1024,128]{1,0:T(8,128)(2,1)}, bf16[1024,128]{1,0:T(8,128)(2,1)S(1)}, u32[]{:S(2)}) copy-start(bf16[1024,128]{1,0:T(8,128)(2,1)S(1)} %get-tuple-element.21) | copy-start | bytes 786436
